TPU v7x, 256 devices: a whole 4x4x8 slice. The times are simulated.
256 devices in a mesh: bead: 16 (over x, z_hi), space: 16 (over z_lo, y, core).
Axes of the slice: x: 4, y: 4, z: 8 (z_hi: 4, z_lo: 2; z = z_hi * 2 + z_lo), core: 2. Of those that a mesh axis runs over, the one named last changes fastest.
Arguments:
- positions: float32 [64, 3, 4096], P('bead', None, 'space'), may hold values from -1 to 17
- species: int32 [4096], P('space'), may hold values from 0 to 1
- neighbors: int32 [32, 4096], P(None, 'space'), may hold values from 0 to 383, as said below
- counts: int32 [4096], P('space'), may hold values from 1 to 32, as said below
- send_rows: int32 [2048], P('space'), may hold values from 0 to 255, as said below
- embed: float32 [2, 128], replicated, may hold values from -6 to 6
- w_radial: float32 [2, 8, 128], replicated, may hold values from -2 to 2
- w_msg: float32 [2, 128, 128], replicated, may hold values from -0.5 to 0.5
- w_upd: float32 [2, 128, 128], replicated, may hold values from -0.5 to 0.5
- w_out: float32 [128], replicated, may hold values from -0.5 to 0.5
Outputs:
- forces: float32 [64, 3, 4096], P('bead', None, 'space')
Inputs may be any that keep to these rules, and one draw needn't show every extreme that they name: `neighbors`: entry n < 256 is the domain's own row n; 256 + s is the s-th left ghost and 320 + s the s-th right ghost. `counts`: slots of an atom below its count are live, the others padding. `send_rows`: each domain's first 64 entries are a permutation of its rows 0 to 63, the next 64 a permutation of its rows 192 to 255.
All inputs are finite; a program needn't handle non-finite values.
Results may differ from a plain program's by a relative error of at most 0.0003.
Values sent between devices are 32-bit elements; how exact they have to be, the bound alone decides.
A program may use at most 64 MiB of HBM per device.

v0:
```python
from functools import partial
import jax
import jax.numpy as jnp
from jax import lax
from jax.sharding import PartitionSpec as P

PC = 16
exact_mode = lax.Precision.HIGHEST
spacing_floor = 0.01
radial_width = 0.2
radial_reach = 1.5
block_rows = 128


def with_halo(block, sides, width):
    for axis, dim in sides:
        count = lax.axis_size(axis)
        forward = [(i, i + 1) for i in range(count - 1)]
        forward.append((count - 1, 0))
        backward = [(target, source) for source, target in forward]
        low = lax.ppermute(
            lax.slice_in_dim(block, block.shape[dim] - width, None, axis=dim), axis, forward
        )
        high = lax.ppermute(lax.slice_in_dim(block, 0, width, axis=dim), axis, backward)
        block = jnp.concatenate([low, block, high], axis=dim)
    return block


def contraction(full_beads, reduced_beads):
    rowpos = jnp.arange(reduced_beads, dtype=jnp.float32)[:, None]
    colpos = jnp.arange(full_beads, dtype=jnp.float32)[None, :]
    phase_gap = rowpos / reduced_beads - colpos / full_beads
    running = jnp.ones_like(phase_gap)
    for harmonic in range(1, reduced_beads // 2):
        running = running + 2.0 * jnp.cos(2.0 * jnp.pi * harmonic * phase_gap)
    running = running + jnp.cos(jnp.pi * reduced_beads * phase_gap)
    return running / full_beads


def silu_slope(argument):
    sigmoid_part = jax.nn.sigmoid(argument)
    return sigmoid_part * (1.0 + argument * (1.0 - sigmoid_part))


def blocked(values, which_axis):
    dims_now = values.shape
    blocks = dims_now[which_axis] // block_rows
    reshaped = values.reshape(
        dims_now[:which_axis] + (blocks, block_rows) + dims_now[which_axis + 1 :]
    )
    return jnp.moveaxis(reshaped, which_axis, 0)


def unblocked(values, which_axis):
    moved_axes = jnp.moveaxis(values, 0, which_axis)
    dims_now = moved_axes.shape
    merged = (dims_now[which_axis] * dims_now[which_axis + 1],)
    return moved_axes.reshape(dims_now[:which_axis] + merged + dims_now[which_axis + 2 :])


def chooser_table(rows, extent):
    columns = lax.broadcasted_iota(jnp.int32, rows.shape + (extent,), rows.ndim)
    return (rows[..., None] == columns).astype(jnp.float32)


def block_message(lent_ext, radial_basis, live_slots, neighbor_rows, radial_map, edge_scale):
    radial_w = jnp.einsum("nbkr,nc->bkrc", radial_basis, radial_map, precision=exact_mode)
    chooser = chooser_table(neighbor_rows, lent_ext.shape[1])
    near_rows = jnp.einsum("kre,bec->bkrc", chooser, lent_ext, precision=exact_mode)
    return edge_scale * jnp.einsum(
        "bkrc,kr->brc", radial_w * near_rows, live_slots, precision=exact_mode
    )


def block_backward(state_pair, inputs, lent_ext, radial_map, edge_scale, want_features):
    grad_lent, grad_points = state_pair
    radial_basis, offsets, displace, distance, live_slots, neighbor_rows, grad_message = inputs
    radial_w = jnp.einsum("nbkr,nc->bkrc", radial_basis, radial_map, precision=exact_mode)
    chooser = chooser_table(neighbor_rows, lent_ext.shape[1])
    near_rows = jnp.einsum("kre,bec->bkrc", chooser, lent_ext, precision=exact_mode)
    weighted = edge_scale * live_slots[None, :, :, None] * grad_message[:, None]
    grad_radial = weighted * near_rows
    grad_basis = jnp.einsum("bkrc,nc->nbkr", grad_radial, radial_map, precision=exact_mode)
    grad_distance = jnp.sum(grad_basis * radial_basis * offsets, axis=0) * (-2.0 / radial_width)
    grad_displace = grad_distance[:, None] * displace / distance[:, None]
    grad_points = grad_points + jnp.einsum(
        "kre,bckr->bce", chooser, grad_displace, precision=exact_mode
    )
    if want_features:
        grad_near = weighted * radial_w
        grad_lent = grad_lent + jnp.einsum(
            "kre,bkrc->bec", chooser, grad_near, precision=exact_mode
        )
    return ((grad_lent, grad_points), -jnp.sum(grad_displace, axis=2))


def on_device(
    positions, species, neighbors, counts, send_rows, embed, w_radial, w_msg, w_upd, w_out
):
    full_dev = positions.shape[0]
    atom_count = positions.shape[2]
    beads_all = full_dev * lax.axis_size("bead")
    reduced_dev = PC // lax.axis_size("bead")
    bead_index = lax.axis_index("bead")
    contract_table = contraction(beads_all, PC)
    own_columns = lax.dynamic_slice_in_dim(contract_table, bead_index * full_dev, full_dev, 1)
    own_table = lax.dynamic_slice_in_dim(contract_table, bead_index * reduced_dev, reduced_dev, 0)
    weights = own_table
    reduced = jnp.einsum(
        "kj,jcn->kcn",
        weights,
        lax.all_gather(positions, "bead", axis=0, tiled=True),
        precision=exact_mode,
    )
    ghost_count = send_rows.shape[0] // 2
    domains = lax.axis_size("space")
    domain = lax.axis_index("space")
    selector = chooser_table(send_rows, atom_count)
    lent_points = jnp.einsum("ga,bca->bcg", selector, reduced, precision=exact_mode)
    lent_species = jnp.dot(selector, species.astype(jnp.float32), precision=exact_mode)
    lent_species = lent_species[None, None]
    outgoing = jnp.concatenate([lent_points, lent_species], axis=1)
    arrived = with_halo(outgoing, (("space", 2),), ghost_count)
    borrowed = jnp.concatenate(
        [arrived[:, :, :ghost_count], arrived[:, :, 3 * ghost_count :]], axis=2
    )
    left_shift = jnp.where(domain == 0, -float(domains), 0.0)
    right_shift = jnp.where(domain == domains - 1, float(domains), 0.0)
    ghost_slot = jnp.arange(2 * ghost_count, dtype=jnp.int32)
    box_shift = jnp.where(ghost_slot < ghost_count, left_shift, right_shift).astype(jnp.float32)
    ghost_points = borrowed[:, :3].at[:, 0].add(box_shift[None])
    ghost_species = borrowed[0, 3]
    ext_points = jnp.concatenate([reduced, ghost_points], axis=2)
    extent = ext_points.shape[2]
    blocks_rows = blocked(neighbors, 1)

    def pick_points(rows_block):
        chooser = chooser_table(rows_block, extent)
        return jnp.einsum("kre,bce->bckr", chooser, ext_points, precision=exact_mode)

    near_points = unblocked(lax.map(pick_points, blocks_rows), 3)
    displace = near_points - reduced[:, :, None, :]
    distance = jnp.sqrt(jnp.sum(displace * displace, axis=1) + spacing_floor)
    basis_count = w_radial.shape[1]
    centers = radial_reach * jnp.arange(basis_count, dtype=jnp.float32) / (basis_count - 1)
    offsets = (distance[None] - centers[:, None, None, None]) / radial_width
    radial_basis = jnp.exp(-offsets * offsets)
    slot_index = lax.broadcasted_iota(jnp.int32, neighbors.shape, 0)
    live_slots = (slot_index < counts[None, :]).astype(jnp.float32)
    edge_scale = neighbors.shape[0] ** (-0.5)
    kinds = jnp.arange(embed.shape[0], dtype=jnp.int32)
    own_onehot = (species[:, None] == kinds[None, :]).astype(jnp.float32)
    ghost_onehot = (ghost_species[:, None] == kinds.astype(jnp.float32)[None, :]).astype(
        jnp.float32
    )
    ext_onehot = jnp.concatenate([own_onehot, ghost_onehot], axis=0)
    hidden = jnp.dot(own_onehot, embed, precision=exact_mode)[None]
    first_table = jnp.dot(embed, w_msg[0], precision=exact_mode)
    blocks_basis = blocked(radial_basis, 3)
    blocks_offsets = blocked(offsets, 3)
    blocks_displace = blocked(displace, 3)
    blocks_distance = blocked(distance, 2)
    blocks_live = blocked(live_slots, 1)
    layer_total = w_msg.shape[0]
    saved = []
    for layer_index in range(layer_total):
        if layer_index == 0:
            first_rows = jnp.dot(ext_onehot, first_table, precision=exact_mode)
            lent_ext = first_rows[None]
        else:
            lent_own = jnp.einsum("bac,cd->bad", hidden, w_msg[layer_index], precision=exact_mode)
            outgoing_rows = jnp.einsum("ga,bac->bgc", selector, lent_own, precision=exact_mode)
            arrived_rows = with_halo(outgoing_rows, (("space", 1),), ghost_count)
            lent_ext = jnp.concatenate(
                [lent_own, arrived_rows[:, :ghost_count], arrived_rows[:, 3 * ghost_count :]],
                axis=1,
            )
        radial_map = w_radial[layer_index]
        per_block = lax.map(
            lambda parts: block_message(
                lent_ext, parts[0], parts[1], parts[2], radial_map, edge_scale
            ),
            (blocks_basis, blocks_live, blocks_rows),
        )
        message = unblocked(per_block, 1)
        update = jnp.einsum("bac,cd->bad", message, w_upd[layer_index], precision=exact_mode)
        saved.append((lent_ext, update))
        hidden = hidden + jax.nn.silu(update)
    grad_hidden = jnp.broadcast_to(w_out[None, None], hidden.shape)
    grad_points = jnp.zeros(ext_points.shape, jnp.float32)
    center_pull = jnp.zeros(reduced.shape, jnp.float32)
    for layer_index in reversed(range(layer_total)):
        lent_ext, update = saved[layer_index]
        grad_update = grad_hidden * silu_slope(update)
        grad_message = jnp.einsum(
            "bac,dc->bad", grad_update, w_upd[layer_index], precision=exact_mode
        )
        want_features = layer_index > 0
        if want_features:
            start_lent = jnp.zeros(lent_ext.shape, jnp.float32)
        else:
            start_lent = jnp.zeros((1,), jnp.float32)
        step_function = partial(
            block_backward,
            lent_ext=lent_ext,
            radial_map=w_radial[layer_index],
            edge_scale=edge_scale,
            want_features=want_features,
        )
        scanned = (
            blocks_basis,
            blocks_offsets,
            blocks_displace,
            blocks_distance,
            blocks_live,
            blocks_rows,
            blocked(grad_message, 1),
        )
        (grad_lent, grad_points), pulls = lax.scan(
            step_function, (start_lent, grad_points), scanned
        )
        center_pull = center_pull + unblocked(pulls, 2)
        if want_features:
            sent_back = with_halo(grad_lent[:, atom_count:], (("space", 1),), ghost_count)
            returned = jnp.concatenate(
                [sent_back[:, :ghost_count], sent_back[:, 3 * ghost_count :]], axis=1
            )
            grad_own = grad_lent[:, :atom_count] + jnp.einsum(
                "ga,bgc->bac", selector, returned, precision=exact_mode
            )
            grad_hidden = grad_hidden + jnp.einsum(
                "bac,dc->bad", grad_own, w_msg[layer_index], precision=exact_mode
            )
    sent_force = with_halo(grad_points[:, :, atom_count:], (("space", 2),), ghost_count)
    returned_force = jnp.concatenate(
        [sent_force[:, :, :ghost_count], sent_force[:, :, 3 * ghost_count :]], axis=2
    )
    energy_grad = (
        grad_points[:, :, :atom_count]
        + center_pull
        + jnp.einsum("ga,bcg->bca", selector, returned_force, precision=exact_mode)
    )
    pull_reduced = -energy_grad
    ratio = float(beads_all) / PC
    weights = own_columns
    return ratio * jnp.einsum(
        "kj,kcn->jcn",
        weights,
        lax.all_gather(pull_reduced, "bead", axis=0, tiled=True),
        precision=exact_mode,
    )


def solution(mesh):
    return jax.shard_map(
        on_device,
        mesh=mesh,
        in_specs=(
            P("bead", None, "space"),
            P("space"),
            P(None, "space"),
            P("space"),
            P("space"),
            P(),
            P(),
            P(),
            P(),
            P(),
        ),
        out_specs=P("bead", None, "space"),
        check_vma=False,
    )
```

profile of v0, /device:TPU:64, one launch (start us, length us, event | category | flops | bytes accessed | tf_op | source)
XLA Modules:
  0.0 223.0 jit_solution(11656162681923624815)
XLA Ops:
  0.0 0.7 copy.41
  0.7 42.8 %all_gather.6 = f32[64,3,256]{2,1,0:T(4,128)S(1)} all-gather(f32[4,3,256]{2,1,0:T(4,128)S(1)} %copy.41), channel_id=1, replica_groups=mesh['bead'=16,'space'=16] {'bead'}, dimensions={0}, use_global_device_ids=true | all-gather | bytes 208896 | tf_op jit(solution)/shard_map/all_gather | solution.py:112
  43.6 0.7 convert_element_type.24
  44.8 0.9 convolution_bitcast_fusion.6
  45.6 0.9 convolution_bitcast_fusion.7
  46.7 3.8 %collective-permute-start.1 = (f32[1,4,64]{2,1,0:T(4,128)S(1)}, f32[1,4,64]{2,1,0:T(4,128)S(1)}, u32[]{:S(2)}, u32[]{:S(2)}) collective-permute-start(f32[1,4,64]{2,1,0:T(4,128)S(1)} %get-tuple-element.553), channel_id=1, source_target_pairs={{1,0},{2,1},{3,2},{4,3},{5,4},{6,5},{7,6},{8,7},{9,8},{10,9},{11,1... | collective-permute-start | bytes 3080 | tf_op jit(solution)/shard_map/ppermute | solution.py:24
  50.6 0.7 iota_compare_fusion.40
  51.2 0.7 fusion.152
  51.9 0.7 slice_bitcast_fusion
  52.6 1.0 fusion.137
  53.7 0.8 reshape.448
  54.9 7.0 %while.58 = (s32[]{:T(128)}, f32[2,1,3,32,128]{4,2,3,1,0:T(4,128)S(1)}, s32[2,32,128]{2,1,0:T(8,128)S(1)}, f32[1,3,384]{2,1,0:T(4,128)S(1)}, s32[]{:T(128)}) while((s32[]{:T(128)}, f32[2,1,3,32,128]{4,2,3,1,0:T(4,128)S(1)}, s32[2,32,128]{2,1,0:T(8,128)S(1)}, f32[1,3,384]{2,1,0:T(4,128)S(1)}, s32[]{:T(128)}) %tuple.106), condition=%wide.region_1.2_spmd, body=%wide.region_0.1_spmd.sunk | while | flops 58195968 | bytes 120901 | solution.py:141
  54.9 3.5 %fusion.252 = f32[2,1,3,32,128]{4,2,3,1,0:T(4,128)S(1)} fusion(f32[2,1,3,32,128]{4,2,3,1,0:T(4,128)S(1)} %get-tuple-element.823, s32[]{:T(128)} %get-tuple-element.822, s32[32,128]{1,0:T(8,128)S(1)} %dynamic-slice_bitcast_fusion.22, f32[1,3,384]{2,1,0:T(4,128)S(1)} %get-tuple-element.830), kind=kOutput, calls=%fused_computation.4.clone.1 | convolution fusion | flops 58195968 | bytes 88068 | tf_op jit(solution)/shard_map/while/body/eval_jaxpr/kre,bce->bckr/dot_general | solution.py:139
  58.4 3.5 %fusion.252 = f32[2,1,3,32,128]{4,2,3,1,0:T(4,128)S(1)} fusion(f32[2,1,3,32,128]{4,2,3,1,0:T(4,128)S(1)} %get-tuple-element.823, s32[]{:T(128)} %get-tuple-element.822, s32[32,128]{1,0:T(8,128)S(1)} %dynamic-slice_bitcast_fusion.22, f32[1,3,384]{2,1,0:T(4,128)S(1)} %get-tuple-element.830), kind=kOutput, calls=%fused_computation.4.clone.1 | convolution fusion | flops 58195968 | bytes 88068 | tf_op jit(solution)/shard_map/while/body/eval_jaxpr/kre,bce->bckr/dot_general | solution.py:139
  62.7 19.7 %while.59 = (s32[]{:T(128)}, f32[2,1,128,128]{3,2,1,0:T(8,128)S(1)}, f32[2,32,128]{2,1,0:T(8,128)S(1)}, f32[2,8,1,32,128]{4,1,3,2,0:T(8,128)S(1)}, f32[8,128]{1,...) while((s32[]{:T(128)}, f32[2,1,128,128]{3,2,1,0:T(8,128)S(1)}, ...), condition=%wide.region_4.5_spmd, body=%wide.region_3.4_spmd.sunk | while | flops 2474655744 | bytes 9048165 | solution.py:179
  62.7 3.4 %fusion.258 = f32[32,128,128]{2,1,0:T(8,128)S(1)} fusion(f32[2,8,1,32,128]{4,1,3,2,0:T(8,128)S(1)} %get-tuple-element.851, s32[]{:T(128)} %get-tuple-element.840, f32[8,128]{1,0:T(8,128)S(1)} %get-tuple-element.852), kind=kOutput, calls=%fused_computation.15.clone.1 | convolution fusion | flops 50331648 | bytes 2232324 | tf_op jit(solution)/shard_map/while/body/eval_jaxpr/nbkr,nc->bkrc/dot_general | solution.py:67
  66.1 3.3 %fusion.259 = f32[32,128,128]{2,1,0:T(8,128)S(1)} fusion(f32[32,128,128]{2,1,0:T(8,128)S(1)} %fusion.258, s32[32,128]{1,0:T(8,128)S(1)} %dynamic-slice_bitcast_fusion.24, f32[1,384,128]{2,1,0:T(8,128)S(1)} %get-tuple-element.854), kind=kOutput, calls=%fused_computation.11.clone.1 | convolution fusion | flops 2418016256 | bytes 4407296 | tf_op jit(solution)/shard_map/while/body/eval_jaxpr/kre,bec->bkrc/dot_general | solution.py:69
  69.6 2.9 %fusion.260 = f32[128,1,128]{2,1,0:T(1,128)S(1)} fusion(f32[32,128,1]{0,2,1:T(1,128)S(1)} %copy.85, f32[32,128,128]{2,1,0:T(8,128)S(1)} %fusion.259), kind=kOutput, calls=%fused_computation.12.clone.1 | convolution fusion | flops 6291456 | bytes 2179072 | tf_op jit(solution)/shard_map/while/body/eval_jaxpr/bkrc,kr->brc/dot_general | solution.py:70
  72.5 3.4 %fusion.258 = f32[32,128,128]{2,1,0:T(8,128)S(1)} fusion(f32[2,8,1,32,128]{4,1,3,2,0:T(8,128)S(1)} %get-tuple-element.851, s32[]{:T(128)} %get-tuple-element.840, f32[8,128]{1,0:T(8,128)S(1)} %get-tuple-element.852), kind=kOutput, calls=%fused_computation.15.clone.1 | convolution fusion | flops 50331648 | bytes 2232324 | tf_op jit(solution)/shard_map/while/body/eval_jaxpr/nbkr,nc->bkrc/dot_general | solution.py:67
  76.0 3.3 %fusion.259 = f32[32,128,128]{2,1,0:T(8,128)S(1)} fusion(f32[32,128,128]{2,1,0:T(8,128)S(1)} %fusion.258, s32[32,128]{1,0:T(8,128)S(1)} %dynamic-slice_bitcast_fusion.24, f32[1,384,128]{2,1,0:T(8,128)S(1)} %get-tuple-element.854), kind=kOutput, calls=%fused_computation.11.clone.1 | convolution fusion | flops 2418016256 | bytes 4407296 | tf_op jit(solution)/shard_map/while/body/eval_jaxpr/kre,bec->bkrc/dot_general | solution.py:69
  79.4 2.9 %fusion.260 = f32[128,1,128]{2,1,0:T(1,128)S(1)} fusion(f32[32,128,1]{0,2,1:T(1,128)S(1)} %copy.85, f32[32,128,128]{2,1,0:T(8,128)S(1)} %fusion.259), kind=kOutput, calls=%fused_computation.12.clone.1 | convolution fusion | flops 6291456 | bytes 2179072 | tf_op jit(solution)/shard_map/while/body/eval_jaxpr/bkrc,kr->brc/dot_general | solution.py:70
  82.7 0.6 copy-done.2
  83.6 1.1 fusion.133
  85.1 4.3 %collective-permute-start.3 = (f32[1,64,128]{2,1,0:T(8,128)S(1)}, f32[1,64,128]{2,1,0:T(8,128)S(1)}, u32[]{:S(2)}, u32[]{:S(2)}) collective-permute-start(f32[1,64,128]{2,1,0:T(8,128)S(1)} %get-tuple-element.538), channel_id=1, source_target_pairs={{1,0},{2,1},{3,2},{4,3},{5,4},{6,5},{7,6},{8,7},{9,8},{10,9},{11,1... | collective-permute-start | bytes 98312 | tf_op jit(solution)/shard_map/ppermute | solution.py:24
  89.4 1.1 collective-permute-done.2
  91.0 0.7 broadcast.295
  91.7 20.9 %while.60 = (s32[]{:T(128)}, f32[2,1,128,128]{3,2,1,0:T(8,128)}, f32[2,32,128]{2,1,0:T(8,128)S(1)}, f32[2,8,1,32,128]{4,1,3,2,0:T(8,128)S(1)}, f32[8,128]{1,0:T(...) while((s32[]{:T(128)}, f32[2,1,128,128]{3,2,1,0:T(8,128)}, ...), condition=%wide.region_6.7_spmd, body=%wide.region_5.6_spmd.sunk | while | flops 2474655744 | bytes 9048673 | solution.py:179
  91.7 3.4 %fusion.266 = f32[32,128,128]{2,1,0:T(8,128)S(1)} fusion(f32[2,8,1,32,128]{4,1,3,2,0:T(8,128)S(1)} %get-tuple-element.875, s32[]{:T(128)} %get-tuple-element.864, f32[8,128]{1,0:T(8,128)S(1)} %get-tuple-element.876), kind=kOutput, calls=%fused_computation.31.clone.1 | convolution fusion | flops 50331648 | bytes 2232324 | tf_op jit(solution)/shard_map/while/body/eval_jaxpr/nbkr,nc->bkrc/dot_general | solution.py:67
  95.2 3.3 %fusion.267 = f32[32,128,128]{2,1,0:T(8,128)S(1)} fusion(f32[32,128,128]{2,1,0:T(8,128)S(1)} %fusion.266, s32[32,128]{1,0:T(8,128)S(1)} %dynamic-slice_bitcast_fusion.26, f32[1,384,128]{2,1,0:T(8,128)S(1)} %get-tuple-element.878), kind=kOutput, calls=%fused_computation.27.clone.1 | convolution fusion | flops 2418016256 | bytes 4407296 | tf_op jit(solution)/shard_map/while/body/eval_jaxpr/kre,bec->bkrc/dot_general | solution.py:69
  98.6 2.9 %fusion.268 = f32[128,1,128]{2,1,0:T(1,128)S(1)} fusion(f32[32,128,1]{0,2,1:T(1,128)S(1)} %copy.87, f32[32,128,128]{2,1,0:T(8,128)S(1)} %fusion.267), kind=kOutput, calls=%fused_computation.28.clone.1 | convolution fusion | flops 6291456 | bytes 2179072 | tf_op jit(solution)/shard_map/while/body/eval_jaxpr/bkrc,kr->brc/dot_general | solution.py:70
  101.5 0.7 bitcast_dynamic-update-slice_fusion.7
  102.2 3.4 %fusion.266 = f32[32,128,128]{2,1,0:T(8,128)S(1)} fusion(f32[2,8,1,32,128]{4,1,3,2,0:T(8,128)S(1)} %get-tuple-element.875, s32[]{:T(128)} %get-tuple-element.864, f32[8,128]{1,0:T(8,128)S(1)} %get-tuple-element.876), kind=kOutput, calls=%fused_computation.31.clone.1 | convolution fusion | flops 50331648 | bytes 2232324 | tf_op jit(solution)/shard_map/while/body/eval_jaxpr/nbkr,nc->bkrc/dot_general | solution.py:67
  105.6 3.3 %fusion.267 = f32[32,128,128]{2,1,0:T(8,128)S(1)} fusion(f32[32,128,128]{2,1,0:T(8,128)S(1)} %fusion.266, s32[32,128]{1,0:T(8,128)S(1)} %dynamic-slice_bitcast_fusion.26, f32[1,384,128]{2,1,0:T(8,128)S(1)} %get-tuple-element.878), kind=kOutput, calls=%fused_computation.27.clone.1 | convolution fusion | flops 2418016256 | bytes 4407296 | tf_op jit(solution)/shard_map/while/body/eval_jaxpr/kre,bec->bkrc/dot_general | solution.py:69
  109.1 2.9 %fusion.268 = f32[128,1,128]{2,1,0:T(1,128)S(1)} fusion(f32[32,128,1]{0,2,1:T(1,128)S(1)} %copy.87, f32[32,128,128]{2,1,0:T(8,128)S(1)} %fusion.267), kind=kOutput, calls=%fused_computation.28.clone.1 | convolution fusion | flops 6291456 | bytes 2179072 | tf_op jit(solution)/shard_map/while/body/eval_jaxpr/bkrc,kr->brc/dot_general | solution.py:70
  112.0 0.6 bitcast_dynamic-update-slice_fusion.7
  112.6 1.2 multiply_multiply_fusion
  114.1 32.4 %while.62 = (s32[]{:T(128)}, f32[1,384,128]{1,2,0:T(8,128)}, f32[1,3,384]{2,1,0:T(4,128)S(1)}, f32[2,1,3,128]{3,2,1,0:T(4,128)S(1)}, f32[2,32,128]{2,1,0:T(8,128...) while((s32[]{:T(128)}, f32[1,384,128]{1,2,0:T(8,128)}, ...), condition=%wide.region_10.11_spmd.clone, body=%wide.region_7.10_spmd.clone.sunk | while | flops 4996204544 | bytes 10068156 | solution.py:219
  114.3 3.4 %fusion.284 = f32[32,128,128]{2,1,0:T(8,128)S(1)} fusion(f32[2,8,1,32,128]{4,1,3,2,0:T(8,128)S(1)} %get-tuple-element.916, s32[]{:T(128)} %get-tuple-element.895, f32[8,128]{1,0:T(8,128)S(1)} %get-tuple-element.917), kind=kOutput, calls=%fused_computation.99.clone.1 | convolution fusion | flops 50331648 | bytes 2232324 | tf_op jit(solution)/shard_map/while/body/eval_jaxpr/nbkr,nc->bkrc/dot_general | solution.py:78
  117.8 4.2 %fusion.285 = f32[1,384,128]{1,2,0:T(8,128)} fusion(s32[32,128]{1,0:T(8,128)S(1)} %dynamic-slice_bitcast_fusion.30, f32[32,128,128]{2,1,0:T(8,128)S(1)} %fusion.284, f32[128,128]{1,0:T(8,128)S(1)} %dynamic-slice_bitcast_fusion.31, f32[32,128]{1,0:T(8,128)S(1)} %multiply_bitcast_fusion.5, f32[1,384,128]{1,2,0:T(8,128)} %get-tuple-element.896, ...), kind=kOutput, calls=%fused_computation.87.clone.1 | convolution fusion | flops 2418638848 | bytes 2588673 | tf_op jit(solution)/shard_map/while/body/eval_jaxpr/kre,bkrc->bec/dot_general | solution.py:91
  122.0 3.2 %fusion.286 = f32[32,128,128]{2,1,0:T(8,128)S(1)} fusion(s32[32,128]{1,0:T(8,128)S(1)} %dynamic-slice_bitcast_fusion.30, f32[1,384,128]{2,1,0:T(8,128)S(1)} %get-tuple-element.919), kind=kOutput, calls=%fused_computation.75.clone.1 | convolution fusion | flops 2417491968 | bytes 2310144 | tf_op jit(solution)/shard_map/while/body/eval_jaxpr/kre,bec->bkrc/dot_general | solution.py:80
  125.2 2.4 %fusion.287 = f32[32,128]{1,0:T(8,128)S(1)} fusion(f32[32,128,128]{2,1,0:T(8,128)S(1)} %fusion.286, f32[128,128]{1,0:T(8,128)S(1)} %dynamic-slice_bitcast_fusion.31, f32[32,128]{1,0:T(8,128)S(1)} %multiply_bitcast_fusion.5, f32[2,8,1,32,128]{4,1,3,2,0:T(8,128)S(1)} %get-tuple-element.920, s32[]{:T(128)} %get-tuple-element.895, ...), kind=kOutput, calls=%fused_computation.91.clone.1 | convolution fusion | flops 51474432 | bytes 2461700 | tf_op jit(solution)/shard_map/while/body/eval_jaxpr/bkrc,nc->nbkr/dot_general | solution.py:83
  127.6 2.2 fusion.288
  129.9 3.4 %fusion.284 = f32[32,128,128]{2,1,0:T(8,128)S(1)} fusion(f32[2,8,1,32,128]{4,1,3,2,0:T(8,128)S(1)} %get-tuple-element.916, s32[]{:T(128)} %get-tuple-element.895, f32[8,128]{1,0:T(8,128)S(1)} %get-tuple-element.917), kind=kOutput, calls=%fused_computation.99.clone.1 | convolution fusion | flops 50331648 | bytes 2232324 | tf_op jit(solution)/shard_map/while/body/eval_jaxpr/nbkr,nc->bkrc/dot_general | solution.py:78
  133.5 5.1 %fusion.285 = f32[1,384,128]{1,2,0:T(8,128)} fusion(s32[32,128]{1,0:T(8,128)S(1)} %dynamic-slice_bitcast_fusion.30, f32[32,128,128]{2,1,0:T(8,128)S(1)} %fusion.284, f32[128,128]{1,0:T(8,128)S(1)} %dynamic-slice_bitcast_fusion.31, f32[32,128]{1,0:T(8,128)S(1)} %multiply_bitcast_fusion.5, f32[1,384,128]{1,2,0:T(8,128)} %get-tuple-element.896, ...), kind=kOutput, calls=%fused_computation.87.clone.1 | convolution fusion | flops 2418638848 | bytes 2588673 | tf_op jit(solution)/shard_map/while/body/eval_jaxpr/kre,bkrc->bec/dot_general | solution.py:91
  138.6 3.2 %fusion.286 = f32[32,128,128]{2,1,0:T(8,128)S(1)} fusion(s32[32,128]{1,0:T(8,128)S(1)} %dynamic-slice_bitcast_fusion.30, f32[1,384,128]{2,1,0:T(8,128)S(1)} %get-tuple-element.919), kind=kOutput, calls=%fused_computation.75.clone.1 | convolution fusion | flops 2417491968 | bytes 2310144 | tf_op jit(solution)/shard_map/while/body/eval_jaxpr/kre,bec->bkrc/dot_general | solution.py:80
  141.8 2.4 %fusion.287 = f32[32,128]{1,0:T(8,128)S(1)} fusion(f32[32,128,128]{2,1,0:T(8,128)S(1)} %fusion.286, f32[128,128]{1,0:T(8,128)S(1)} %dynamic-slice_bitcast_fusion.31, f32[32,128]{1,0:T(8,128)S(1)} %multiply_bitcast_fusion.5, f32[2,8,1,32,128]{4,1,3,2,0:T(8,128)S(1)} %get-tuple-element.920, s32[]{:T(128)} %get-tuple-element.895, ...), kind=kOutput, calls=%fused_computation.91.clone.1 | convolution fusion | flops 51474432 | bytes 2461700 | tf_op jit(solution)/shard_map/while/body/eval_jaxpr/bkrc,nc->nbkr/dot_general | solution.py:83
  144.2 2.2 fusion.288
  146.5 1.0 fusion.195
  147.8 3.9 %collective-permute-start.5 = (f32[1,64,128]{1,2,0:T(8,128)S(1)}, f32[1,64,128]{1,2,0:T(8,128)S(1)}, u32[]{:S(2)}, u32[]{:S(2)}) collective-permute-start(f32[1,64,128]{1,2,0:T(8,128)S(1)} %get-tuple-element.536), channel_id=1, source_target_pairs={{1,0},{2,1},{3,2},{4,3},{5,4},{6,5},{7,6},{8,7},{9,8},{10,9},{11,1... | collective-permute-start | bytes 98312 | tf_op jit(solution)/shard_map/ppermute | solution.py:24
  151.7 1.9 collective-permute-done.4
  153.6 1.2 fusion.114
  154.8 1.3 fusion.112
  156.2 1.1 convolution_bitcast_fusion.1
  157.3 16.0 %while.61 = (s32[]{:T(128)}, f32[1,3,384]{2,1,0:T(4,128)S(1)}, f32[2,1,3,128]{3,2,1,0:T(4,128)S(1)}, f32[2,32,128]{2,1,0:T(8,128)S(1)}, f32[2,1,128,128]{3,2,1,0...) while((s32[]{:T(128)}, f32[1,3,384]{2,1,0:T(4,128)S(1)}, ...), condition=%wide.region_14.15_spmd, body=%wide.region_11.14_spmd.sunk | while | flops 2527233024 | bytes 5247133 | solution.py:219
  157.3 3.3 %fusion.273 = f32[32,128,128]{2,1,0:T(8,128)S(1)} fusion(s32[32,128]{1,0:T(8,128)S(1)} %dynamic-slice_bitcast_fusion.27, f32[1,384,128]{2,1,0:T(8,128)S(1)} %get-tuple-element.957), kind=kOutput, calls=%fused_computation.41.clone.1 | convolution fusion | flops 2417491968 | bytes 2310144 | tf_op jit(solution)/shard_map/while/body/eval_jaxpr/kre,bec->bkrc/dot_general | solution.py:80
  160.6 2.3 %fusion.274 = f32[32,128]{1,0:T(8,128)S(1)} fusion(f32[32,128,128]{2,1,0:T(8,128)S(1)} %fusion.273, f32[128,128]{1,0:T(8,128)S(1)} %dynamic-slice_bitcast_fusion.29, f32[32,128]{1,0:T(8,128)S(1)} %multiply_bitcast_fusion.4, f32[2,8,1,32,128]{4,1,3,2,0:T(8,128)S(1)} %get-tuple-element.960, s32[]{:T(128)} %get-tuple-element.938, ...), kind=kOutput, calls=%fused_computation.51.clone.1 | convolution fusion | flops 51474432 | bytes 2461700 | tf_op jit(solution)/shard_map/while/body/eval_jaxpr/bkrc,nc->nbkr/dot_general | solution.py:83
  163.1 2.2 fusion.275
  165.3 3.3 %fusion.273 = f32[32,128,128]{2,1,0:T(8,128)S(1)} fusion(s32[32,128]{1,0:T(8,128)S(1)} %dynamic-slice_bitcast_fusion.27, f32[1,384,128]{2,1,0:T(8,128)S(1)} %get-tuple-element.957), kind=kOutput, calls=%fused_computation.41.clone.1 | convolution fusion | flops 2417491968 | bytes 2310144 | tf_op jit(solution)/shard_map/while/body/eval_jaxpr/kre,bec->bkrc/dot_general | solution.py:80
  168.6 2.3 %fusion.274 = f32[32,128]{1,0:T(8,128)S(1)} fusion(f32[32,128,128]{2,1,0:T(8,128)S(1)} %fusion.273, f32[128,128]{1,0:T(8,128)S(1)} %dynamic-slice_bitcast_fusion.29, f32[32,128]{1,0:T(8,128)S(1)} %multiply_bitcast_fusion.4, f32[2,8,1,32,128]{4,1,3,2,0:T(8,128)S(1)} %get-tuple-element.960, s32[]{:T(128)} %get-tuple-element.938, ...), kind=kOutput, calls=%fused_computation.51.clone.1 | convolution fusion | flops 51474432 | bytes 2461700 | tf_op jit(solution)/shard_map/while/body/eval_jaxpr/bkrc,nc->nbkr/dot_general | solution.py:83
  171.1 2.2 fusion.275
  173.4 4.0 %collective-permute-start.7 = (f32[1,3,64]{2,1,0:T(4,128)S(1)}, f32[1,3,64]{2,1,0:T(4,128)S(1)}, u32[]{:S(2)}, u32[]{:S(2)}) collective-permute-start(f32[1,3,64]{2,1,0:T(4,128)S(1)} %get-tuple-element.546), channel_id=1, source_target_pairs={{1,0},{2,1},{3,2},{4,3},{5,4},{6,5},{7,6},{8,7},{9,8},{10,9},{11,1... | collective-permute-start | bytes 2312 | tf_op jit(solution)/shard_map/ppermute | solution.py:24
  177.3 1.2 collective-permute-done.6
  178.9 43.0 %all_gather.7 = f32[16,3,256]{2,1,0:T(4,128)S(1)} all-gather(f32[1,3,256]{2,1,0:T(4,128)S(1)} %fusion.116), channel_id=1, replica_groups=mesh['bead'=16,'space'=16] {'bead'}, dimensions={0}, use_global_device_ids=true | all-gather | bytes 52224 | tf_op jit(solution)/shard_map/all_gather | solution.py:249
  221.9 0.9 convolution_multiply_fusion
  (98 shorter events, 5.3 us)
Async XLA Ops:
  0.0 52.6 %copy-start = (f32[2,128]{1,0:T(2,128)S(1)}, f32[2,128]{1,0:T(2,128)}, u32[]{:S(2)}) copy-start(f32[2,128]{1,0:T(2,128)} %param.27) | copy-start | bytes 3076
  46.7 7.8 %collective-permute-start = (f32[1,4,64]{2,1,0:T(4,128)S(1)}, f32[1,4,64]{2,1,0:T(4,128)S(1)}, u32[]{:S(2)}, u32[]{:S(2)}) collective-permute-start(f32[1,4,64]{2,1,0:T(4,128)S(1)} %get-tuple-element.552), channel_id=1, source_target_pairs={{0,1},{1,2},{2,3},{3,4},{4,5},{5,6},{6,7},{7,8},{8,9},{9,10},{10,1... | collective-permute-start | bytes 3080 | tf_op jit(solution)/shard_map/ppermute | solution.py:21
  46.7 7.8 %collective-permute-start.1 = (f32[1,4,64]{2,1,0:T(4,128)S(1)}, f32[1,4,64]{2,1,0:T(4,128)S(1)}, u32[]{:S(2)}, u32[]{:S(2)}) collective-permute-start(f32[1,4,64]{2,1,0:T(4,128)S(1)} %get-tuple-element.553), channel_id=1, source_target_pairs={{1,0},{2,1},{3,2},{4,3},{5,4},{6,5},{7,6},{8,7},{9,8},{10,9},{11,1... | collective-permute-start | bytes 3080 | tf_op jit(solution)/shard_map/ppermute | solution.py:24
  62.6 19.7 %copy-start.1 = (f32[2,128,128]{2,1,0:T(8,128)S(1)}, f32[2,128,128]{2,1,0:T(8,128)}, u32[]{:S(2)}) copy-start(f32[2,128,128]{2,1,0:T(8,128)} %param.30) | copy-start | bytes 393220
  62.6 20.6 %copy-start.3 = (s32[256]{0:T(256)S(1)}, s32[256]{0:T(256)}, u32[]{:S(2)}) copy-start(s32[256]{0:T(256)} %param.23) | copy-start | bytes 3076
  62.7 22.0 %copy-start.4 = (s32[128]{0:T(128)S(1)}, s32[128]{0:T(128)}, u32[]{:S(2)}) copy-start(s32[128]{0:T(128)} %param.26) | copy-start | bytes 1540
  82.6 0.6 copy-start.2
  85.0 5.5 %collective-permute-start.2 = (f32[1,64,128]{2,1,0:T(8,128)S(1)}, f32[1,64,128]{2,1,0:T(8,128)S(1)}, u32[]{:S(2)}, u32[]{:S(2)}) collective-permute-start(f32[1,64,128]{2,1,0:T(8,128)S(1)} %get-tuple-element.537), channel_id=1, source_target_pairs={{0,1},{1,2},{2,3},{3,4},{4,5},{5,6},{6,7},{7,8},{8,9},{9,10},{10,1... | collective-permute-start | bytes 98312 | tf_op jit(solution)/shard_map/ppermute | solution.py:21
  85.1 5.9 %collective-permute-start.3 = (f32[1,64,128]{2,1,0:T(8,128)S(1)}, f32[1,64,128]{2,1,0:T(8,128)S(1)}, u32[]{:S(2)}, u32[]{:S(2)}) collective-permute-start(f32[1,64,128]{2,1,0:T(8,128)S(1)} %get-tuple-element.538), channel_id=1, source_target_pairs={{1,0},{2,1},{3,2},{4,3},{5,4},{6,5},{7,6},{8,7},{9,8},{10,9},{11,1... | collective-permute-start | bytes 98312 | tf_op jit(solution)/shard_map/ppermute | solution.py:24
  91.7 20.9 %copy-start.5 = (f32[128]{0:T(128)S(1)}, f32[128]{0:T(128)}, u32[]{:S(2)}) copy-start(f32[128]{0:T(128)} %param.31) | copy-start | bytes 1540
  147.5 6.1 %collective-permute-start.4 = (f32[1,64,128]{1,2,0:T(8,128)S(1)}, f32[1,64,128]{1,2,0:T(8,128)S(1)}, u32[]{:S(2)}, u32[]{:S(2)}) collective-permute-start(f32[1,64,128]{1,2,0:T(8,128)S(1)} %get-tuple-element.535), channel_id=1, source_target_pairs={{0,1},{1,2},{2,3},{3,4},{4,5},{5,6},{6,7},{7,8},{8,9},{9,10},{10,1... | collective-permute-start | bytes 98312 | tf_op jit(solution)/shard_map/ppermute | solution.py:21
  147.8 5.8 %collective-permute-start.5 = (f32[1,64,128]{1,2,0:T(8,128)S(1)}, f32[1,64,128]{1,2,0:T(8,128)S(1)}, u32[]{:S(2)}, u32[]{:S(2)}) collective-permute-start(f32[1,64,128]{1,2,0:T(8,128)S(1)} %get-tuple-element.536), channel_id=1, source_target_pairs={{1,0},{2,1},{3,2},{4,3},{5,4},{6,5},{7,6},{8,7},{9,8},{10,9},{11,1... | collective-permute-start | bytes 98312 | tf_op jit(solution)/shard_map/ppermute | solution.py:24
  173.3 5.2 %collective-permute-start.6 = (f32[1,3,64]{2,1,0:T(4,128)S(1)}, f32[1,3,64]{2,1,0:T(4,128)S(1)}, u32[]{:S(2)}, u32[]{:S(2)}) collective-permute-start(f32[1,3,64]{2,1,0:T(4,128)S(1)} %get-tuple-element.545), channel_id=1, source_target_pairs={{0,1},{1,2},{2,3},{3,4},{4,5},{5,6},{6,7},{7,8},{8,9},{9,10},{10,1... | collective-permute-start | bytes 2312 | tf_op jit(solution)/shard_map/ppermute | solution.py:21
  173.4 5.3 %collective-permute-start.7 = (f32[1,3,64]{2,1,0:T(4,128)S(1)}, f32[1,3,64]{2,1,0:T(4,128)S(1)}, u32[]{:S(2)}, u32[]{:S(2)}) collective-permute-start(f32[1,3,64]{2,1,0:T(4,128)S(1)} %get-tuple-element.546), channel_id=1, source_target_pairs={{1,0},{2,1},{3,2},{4,3},{5,4},{6,5},{7,6},{8,7},{9,8},{10,9},{11,1... | collective-permute-start | bytes 2312 | tf_op jit(solution)/shard_map/ppermute | solution.py:24
where the time goes:
time: 226 us; the launch traced here: 223 us
  matrix products  104 us (46%)
  blocking collectives  85.8 us (38%)
  starting transfers between devices  16.5 us (7%)
  local copies, waits for them, and re-layouts  5.61 us (2%)
  waiting for transfers between devices  4.79 us (2%)
  other arithmetic  4.56 us (2%)
    all_gather x1, blocking collectives, on_device(): lax.all_gather(pull_reduced, 'bead', axis=0, tiled=True)  43 us
    all_gather x1, blocking collectives, on_device(): lax.all_gather(positions, 'bead', axis=0, tiled=True)  42.8 us
    ppermute x4, starting transfers between devices, with_halo(): lax.ppermute(lax.slice_in_dim(block, 0, width, axis=dim), axis, backward)  16.1 us
    dot_general x4, matrix products, block_message(): jnp.einsum('nbkr,nc->bkrc', radial_basis, radial_map, precision=exact_mode)  13.8 us
    dot_general x4, matrix products, block_message(): jnp.einsum('kre,bec->bkrc', chooser, lent_ext, precision=exact_mode)  13.3 us
    dot_general x4, matrix products, block_backward(): jnp.einsum('kre,bec->bkrc', chooser, lent_ext, precision=exact_mode)  13 us
    dot_general x4, matrix products, block_message(): jnp.einsum('bkrc,kr->brc', radial_w * near_rows, live_slots, precision=ex...  11.6 us
    dot_general x4, matrix products, block_backward(): jnp.einsum('bkrc,nc->nbkr', grad_radial, radial_map, precision=exact_mode)  9.4 us
  transfers between devices with their start and end apart: 8, of which 5 were waited for; matrix products, arithmetic and copies ran while one was open for 2% of the time, Pallas kernels for 0%

commit v1 on v0

--- a/solution.py
+++ b/solution.py
@@ -243,10 +243,19 @@
     pull_reduced = -energy_grad
     ratio = float(beads_all) / PC
     weights = own_columns
+    compute_clusters = lambda original, bus_axis: jnp.concatenate(
+        jax.lax.all_to_all(
+            jnp.stack([original] * jax.lax.axis_size(bus_axis), 0),
+            axis_name=bus_axis,
+            split_axis=0,
+            concat_axis=0,
+        ),
+        0,
+    )
     return ratio * jnp.einsum(
         "kj,kcn->jcn",
         weights,
-        lax.all_gather(pull_reduced, "bead", axis=0, tiled=True),
+        compute_clusters(pull_reduced, bus_axis="bead"),
         precision=exact_mode,
     )
 

time: 226 us -> 202 us (0.89)
  the two profiles are of different devices: /device:TPU:64 before, /device:TPU:25 now
where the time goes in v1:
time: 202 us; the launch traced here: 199 us
  matrix products  104 us (51%)
  blocking collectives  40.9 us (20%)
  waiting for transfers between devices  25.6 us (13%)
  starting transfers between devices  16.2 us (8%)
  local copies, waits for them, and re-layouts  6.29 us (3%)
  other arithmetic  4.54 us (2%)
    all_gather x1, blocking collectives, on_device(): lax.all_gather(positions, 'bead', axis=0, tiled=True)  40.9 us
    ppermute x4, waiting for transfers between devices, with_halo(): lax.ppermute(lax.slice_in_dim(block, 0, width, axis=dim), axis, backward)  14.7 us
    dot_general x4, matrix products, block_message(): jnp.einsum('nbkr,nc->bkrc', radial_basis, radial_map, precision=exact_mode)  13.8 us
    dot_general x4, matrix products, block_message(): jnp.einsum('kre,bec->bkrc', chooser, lent_ext, precision=exact_mode)  13.3 us
    dot_general x4, matrix products, block_backward(): jnp.einsum('kre,bec->bkrc', chooser, lent_ext, precision=exact_mode)  13 us
    dot_general x4, matrix products, block_message(): jnp.einsum('bkrc,kr->brc', radial_w * near_rows, live_slots, precision=ex...  11.6 us
    ppermute x4, starting transfers between devices, with_halo(): lax.ppermute(lax.slice_in_dim(block, block.shape[dim] - width, None, axis...  11.2 us
    dot_general x4, matrix products, block_backward(): jnp.einsum('bkrc,nc->nbkr', grad_radial, radial_map, precision=exact_mode)  9.4 us
  transfers between devices with their start and end apart: 9, of which 8 were waited for; matrix products, arithmetic and copies ran while one was open for 2% of the time, Pallas kernels for 0%

profile of v1, /device:TPU:25, one launch (start us, length us, event | category | flops | bytes accessed | tf_op | source)
XLA Modules:
  0.0 199.1 jit_solution(6911686071572154424)
XLA Ops:
  0.0 0.7 copy.51
  0.7 40.9 %all_gather.3 = f32[64,3,256]{2,1,0:T(4,128)S(1)} all-gather(f32[4,3,256]{2,1,0:T(4,128)S(1)} %copy.51), channel_id=1, replica_groups=mesh['bead'=16,'space'=16] {'bead'}, dimensions={0}, use_global_device_ids=true | all-gather | bytes 208896 | tf_op jit(solution)/shard_map/all_gather | solution.py:112
  41.6 0.7 convert_element_type.24
  42.8 0.9 convolution_bitcast_fusion.6
  43.7 0.9 convolution_bitcast_fusion.7
  44.7 8.1 %collective-permute-start = (f32[1,4,64]{2,1,0:T(4,128)S(1)}, f32[1,4,64]{2,1,0:T(4,128)S(1)}, u32[]{:S(2)}, u32[]{:S(2)}) collective-permute-start(f32[1,4,64]{2,1,0:T(4,128)S(1)} %get-tuple-element.595), channel_id=1, source_target_pairs={{0,1},{1,2},{2,3},{3,4},{4,5},{5,6},{6,7},{7,8},{8,9},{9,10},{10,1... | collective-permute-start | bytes 3080 | tf_op jit(solution)/shard_map/ppermute | solution.py:21
  52.8 0.7 iota_compare_fusion.40
  53.5 0.7 fusion.154
  54.2 0.7 slice_bitcast_fusion
  54.9 1.0 fusion.138
  55.9 0.8 reshape.454
  56.7 1.2 collective-permute-done.1
  58.3 7.0 %while.58 = (s32[]{:T(128)}, f32[2,1,3,32,128]{4,2,3,1,0:T(4,128)S(1)}, s32[2,32,128]{2,1,0:T(8,128)S(1)}, f32[1,3,384]{2,1,0:T(4,128)S(1)}, s32[]{:T(128)}) while((s32[]{:T(128)}, f32[2,1,3,32,128]{4,2,3,1,0:T(4,128)S(1)}, s32[2,32,128]{2,1,0:T(8,128)S(1)}, f32[1,3,384]{2,1,0:T(4,128)S(1)}, s32[]{:T(128)}) %tuple.111), condition=%wide.region_1.2_spmd, body=%wide.region_0.1_spmd.sunk | while | flops 58195968 | bytes 120901 | solution.py:141
  58.4 3.5 %fusion.254 = f32[2,1,3,32,128]{4,2,3,1,0:T(4,128)S(1)} fusion(f32[2,1,3,32,128]{4,2,3,1,0:T(4,128)S(1)} %get-tuple-element.866, s32[]{:T(128)} %get-tuple-element.865, s32[32,128]{1,0:T(8,128)S(1)} %dynamic-slice_bitcast_fusion.22, f32[1,3,384]{2,1,0:T(4,128)S(1)} %get-tuple-element.873), kind=kOutput, calls=%fused_computation.4.clone.1 | convolution fusion | flops 58195968 | bytes 88068 | tf_op jit(solution)/shard_map/while/body/eval_jaxpr/kre,bce->bckr/dot_general | solution.py:139
  61.9 3.5 %fusion.254 = f32[2,1,3,32,128]{4,2,3,1,0:T(4,128)S(1)} fusion(f32[2,1,3,32,128]{4,2,3,1,0:T(4,128)S(1)} %get-tuple-element.866, s32[]{:T(128)} %get-tuple-element.865, s32[32,128]{1,0:T(8,128)S(1)} %dynamic-slice_bitcast_fusion.22, f32[1,3,384]{2,1,0:T(4,128)S(1)} %get-tuple-element.873), kind=kOutput, calls=%fused_computation.4.clone.1 | convolution fusion | flops 58195968 | bytes 88068 | tf_op jit(solution)/shard_map/while/body/eval_jaxpr/kre,bce->bckr/dot_general | solution.py:139
  66.1 19.7 %while.59 = (s32[]{:T(128)}, f32[2,1,128,128]{3,2,1,0:T(8,128)S(1)}, f32[2,32,128]{2,1,0:T(8,128)S(1)}, f32[2,8,1,32,128]{4,1,3,2,0:T(8,128)S(1)}, f32[8,128]{1,...) while((s32[]{:T(128)}, f32[2,1,128,128]{3,2,1,0:T(8,128)S(1)}, ...), condition=%wide.region_4.5_spmd, body=%wide.region_3.4_spmd.sunk | while | flops 2474655744 | bytes 9048165 | solution.py:179
  66.1 3.4 %fusion.260 = f32[32,128,128]{2,1,0:T(8,128)S(1)} fusion(f32[2,8,1,32,128]{4,1,3,2,0:T(8,128)S(1)} %get-tuple-element.894, s32[]{:T(128)} %get-tuple-element.883, f32[8,128]{1,0:T(8,128)S(1)} %get-tuple-element.895), kind=kOutput, calls=%fused_computation.15.clone.1 | convolution fusion | flops 50331648 | bytes 2232324 | tf_op jit(solution)/shard_map/while/body/eval_jaxpr/nbkr,nc->bkrc/dot_general | solution.py:67
  69.6 3.3 %fusion.261 = f32[32,128,128]{2,1,0:T(8,128)S(1)} fusion(f32[32,128,128]{2,1,0:T(8,128)S(1)} %fusion.260, s32[32,128]{1,0:T(8,128)S(1)} %dynamic-slice_bitcast_fusion.24, f32[1,384,128]{2,1,0:T(8,128)S(1)} %get-tuple-element.897), kind=kOutput, calls=%fused_computation.11.clone.1 | convolution fusion | flops 2418016256 | bytes 4407296 | tf_op jit(solution)/shard_map/while/body/eval_jaxpr/kre,bec->bkrc/dot_general | solution.py:69
  73.0 2.9 %fusion.262 = f32[128,1,128]{2,1,0:T(1,128)S(1)} fusion(f32[32,128,1]{0,2,1:T(1,128)S(1)} %copy.97, f32[32,128,128]{2,1,0:T(8,128)S(1)} %fusion.261), kind=kOutput, calls=%fused_computation.12.clone.1 | convolution fusion | flops 6291456 | bytes 2179072 | tf_op jit(solution)/shard_map/while/body/eval_jaxpr/bkrc,kr->brc/dot_general | solution.py:70
  76.0 3.4 %fusion.260 = f32[32,128,128]{2,1,0:T(8,128)S(1)} fusion(f32[2,8,1,32,128]{4,1,3,2,0:T(8,128)S(1)} %get-tuple-element.894, s32[]{:T(128)} %get-tuple-element.883, f32[8,128]{1,0:T(8,128)S(1)} %get-tuple-element.895), kind=kOutput, calls=%fused_computation.15.clone.1 | convolution fusion | flops 50331648 | bytes 2232324 | tf_op jit(solution)/shard_map/while/body/eval_jaxpr/nbkr,nc->bkrc/dot_general | solution.py:67
  79.4 3.3 %fusion.261 = f32[32,128,128]{2,1,0:T(8,128)S(1)} fusion(f32[32,128,128]{2,1,0:T(8,128)S(1)} %fusion.260, s32[32,128]{1,0:T(8,128)S(1)} %dynamic-slice_bitcast_fusion.24, f32[1,384,128]{2,1,0:T(8,128)S(1)} %get-tuple-element.897), kind=kOutput, calls=%fused_computation.11.clone.1 | convolution fusion | flops 2418016256 | bytes 4407296 | tf_op jit(solution)/shard_map/while/body/eval_jaxpr/kre,bec->bkrc/dot_general | solution.py:69
  82.9 2.9 %fusion.262 = f32[128,1,128]{2,1,0:T(1,128)S(1)} fusion(f32[32,128,1]{0,2,1:T(1,128)S(1)} %copy.97, f32[32,128,128]{2,1,0:T(8,128)S(1)} %fusion.261), kind=kOutput, calls=%fused_computation.12.clone.1 | convolution fusion | flops 6291456 | bytes 2179072 | tf_op jit(solution)/shard_map/while/body/eval_jaxpr/bkrc,kr->brc/dot_general | solution.py:70
  87.0 1.1 fusion.134
  88.4 2.8 %collective-permute-start.2 = (f32[1,64,128]{2,1,0:T(8,128)S(1)}, f32[1,64,128]{2,1,0:T(8,128)S(1)}, u32[]{:S(2)}, u32[]{:S(2)}) collective-permute-start(f32[1,64,128]{2,1,0:T(8,128)S(1)} %get-tuple-element.580), channel_id=1, source_target_pairs={{0,1},{1,2},{2,3},{3,4},{4,5},{5,6},{6,7},{7,8},{8,9},{9,10},{10,1... | collective-permute-start | bytes 98312 | tf_op jit(solution)/shard_map/ppermute | solution.py:21
  92.2 4.9 %collective-permute-done.3 = f32[1,64,128]{2,1,0:T(8,128)S(1)} collective-permute-done((f32[1,64,128]{2,1,0:T(8,128)S(1)}, f32[1,64,128]{2,1,0:T(8,128)S(1)}, u32[]{:S(2)}, u32[]{:S(2)}) %collective-permute-start.3) | collective-permute-done | bytes 32800 | tf_op jit(solution)/shard_map/ppermute | solution.py:24
  97.2 0.7 broadcast.298
  97.8 20.9 %while.60 = (s32[]{:T(128)}, f32[2,1,128,128]{3,2,1,0:T(8,128)}, f32[2,32,128]{2,1,0:T(8,128)S(1)}, f32[2,8,1,32,128]{4,1,3,2,0:T(8,128)S(1)}, f32[8,128]{1,0:T(...) while((s32[]{:T(128)}, f32[2,1,128,128]{3,2,1,0:T(8,128)}, ...), condition=%wide.region_6.7_spmd, body=%wide.region_5.6_spmd.sunk | while | flops 2474655744 | bytes 9048673 | solution.py:179
  97.8 3.4 %fusion.268 = f32[32,128,128]{2,1,0:T(8,128)S(1)} fusion(f32[2,8,1,32,128]{4,1,3,2,0:T(8,128)S(1)} %get-tuple-element.918, s32[]{:T(128)} %get-tuple-element.907, f32[8,128]{1,0:T(8,128)S(1)} %get-tuple-element.919), kind=kOutput, calls=%fused_computation.31.clone.1 | convolution fusion | flops 50331648 | bytes 2232324 | tf_op jit(solution)/shard_map/while/body/eval_jaxpr/nbkr,nc->bkrc/dot_general | solution.py:67
  101.3 3.3 %fusion.269 = f32[32,128,128]{2,1,0:T(8,128)S(1)} fusion(f32[32,128,128]{2,1,0:T(8,128)S(1)} %fusion.268, s32[32,128]{1,0:T(8,128)S(1)} %dynamic-slice_bitcast_fusion.26, f32[1,384,128]{2,1,0:T(8,128)S(1)} %get-tuple-element.921), kind=kOutput, calls=%fused_computation.27.clone.1 | convolution fusion | flops 2418016256 | bytes 4407296 | tf_op jit(solution)/shard_map/while/body/eval_jaxpr/kre,bec->bkrc/dot_general | solution.py:69
  104.7 2.9 %fusion.270 = f32[128,1,128]{2,1,0:T(1,128)S(1)} fusion(f32[32,128,1]{0,2,1:T(1,128)S(1)} %copy.99, f32[32,128,128]{2,1,0:T(8,128)S(1)} %fusion.269), kind=kOutput, calls=%fused_computation.28.clone.1 | convolution fusion | flops 6291456 | bytes 2179072 | tf_op jit(solution)/shard_map/while/body/eval_jaxpr/bkrc,kr->brc/dot_general | solution.py:70
  108.3 3.4 %fusion.268 = f32[32,128,128]{2,1,0:T(8,128)S(1)} fusion(f32[2,8,1,32,128]{4,1,3,2,0:T(8,128)S(1)} %get-tuple-element.918, s32[]{:T(128)} %get-tuple-element.907, f32[8,128]{1,0:T(8,128)S(1)} %get-tuple-element.919), kind=kOutput, calls=%fused_computation.31.clone.1 | convolution fusion | flops 50331648 | bytes 2232324 | tf_op jit(solution)/shard_map/while/body/eval_jaxpr/nbkr,nc->bkrc/dot_general | solution.py:67
  111.7 3.3 %fusion.269 = f32[32,128,128]{2,1,0:T(8,128)S(1)} fusion(f32[32,128,128]{2,1,0:T(8,128)S(1)} %fusion.268, s32[32,128]{1,0:T(8,128)S(1)} %dynamic-slice_bitcast_fusion.26, f32[1,384,128]{2,1,0:T(8,128)S(1)} %get-tuple-element.921), kind=kOutput, calls=%fused_computation.27.clone.1 | convolution fusion | flops 2418016256 | bytes 4407296 | tf_op jit(solution)/shard_map/while/body/eval_jaxpr/kre,bec->bkrc/dot_general | solution.py:69
  115.2 2.9 %fusion.270 = f32[128,1,128]{2,1,0:T(1,128)S(1)} fusion(f32[32,128,1]{0,2,1:T(1,128)S(1)} %copy.99, f32[32,128,128]{2,1,0:T(8,128)S(1)} %fusion.269), kind=kOutput, calls=%fused_computation.28.clone.1 | convolution fusion | flops 6291456 | bytes 2179072 | tf_op jit(solution)/shard_map/while/body/eval_jaxpr/bkrc,kr->brc/dot_general | solution.py:70
  118.7 1.2 multiply_multiply_fusion
  120.2 32.4 %while.62 = (s32[]{:T(128)}, f32[1,384,128]{1,2,0:T(8,128)}, f32[1,3,384]{2,1,0:T(4,128)S(1)}, f32[2,1,3,128]{3,2,1,0:T(4,128)S(1)}, f32[2,32,128]{2,1,0:T(8,128...) while((s32[]{:T(128)}, f32[1,384,128]{1,2,0:T(8,128)}, ...), condition=%wide.region_10.11_spmd.clone, body=%wide.region_7.10_spmd.clone.sunk | while | flops 4996204544 | bytes 10068156 | solution.py:219
  120.4 3.4 %fusion.286 = f32[32,128,128]{2,1,0:T(8,128)S(1)} fusion(f32[2,8,1,32,128]{4,1,3,2,0:T(8,128)S(1)} %get-tuple-element.959, s32[]{:T(128)} %get-tuple-element.938, f32[8,128]{1,0:T(8,128)S(1)} %get-tuple-element.960), kind=kOutput, calls=%fused_computation.99.clone.1 | convolution fusion | flops 50331648 | bytes 2232324 | tf_op jit(solution)/shard_map/while/body/eval_jaxpr/nbkr,nc->bkrc/dot_general | solution.py:78
  123.9 4.2 %fusion.287 = f32[1,384,128]{1,2,0:T(8,128)} fusion(s32[32,128]{1,0:T(8,128)S(1)} %dynamic-slice_bitcast_fusion.30, f32[32,128,128]{2,1,0:T(8,128)S(1)} %fusion.286, f32[128,128]{1,0:T(8,128)S(1)} %dynamic-slice_bitcast_fusion.31, f32[32,128]{1,0:T(8,128)S(1)} %multiply_bitcast_fusion.5, f32[1,384,128]{1,2,0:T(8,128)} %get-tuple-element.939, ...), kind=kOutput, calls=%fused_computation.87.clone.1 | convolution fusion | flops 2418638848 | bytes 2588673 | tf_op jit(solution)/shard_map/while/body/eval_jaxpr/kre,bkrc->bec/dot_general | solution.py:91
  128.1 3.2 %fusion.288 = f32[32,128,128]{2,1,0:T(8,128)S(1)} fusion(s32[32,128]{1,0:T(8,128)S(1)} %dynamic-slice_bitcast_fusion.30, f32[1,384,128]{2,1,0:T(8,128)S(1)} %get-tuple-element.962), kind=kOutput, calls=%fused_computation.75.clone.1 | convolution fusion | flops 2417491968 | bytes 2310144 | tf_op jit(solution)/shard_map/while/body/eval_jaxpr/kre,bec->bkrc/dot_general | solution.py:80
  131.4 2.4 %fusion.289 = f32[32,128]{1,0:T(8,128)S(1)} fusion(f32[32,128,128]{2,1,0:T(8,128)S(1)} %fusion.288, f32[128,128]{1,0:T(8,128)S(1)} %dynamic-slice_bitcast_fusion.31, f32[32,128]{1,0:T(8,128)S(1)} %multiply_bitcast_fusion.5, f32[2,8,1,32,128]{4,1,3,2,0:T(8,128)S(1)} %get-tuple-element.963, s32[]{:T(128)} %get-tuple-element.938, ...), kind=kOutput, calls=%fused_computation.91.clone.1 | convolution fusion | flops 51474432 | bytes 2461700 | tf_op jit(solution)/shard_map/while/body/eval_jaxpr/bkrc,nc->nbkr/dot_general | solution.py:83
  133.8 2.2 %fusion.290 = f32[1,3,384]{2,1,0:T(4,128)S(1)} fusion(s32[32,128]{1,0:T(8,128)S(1)} %dynamic-slice_bitcast_fusion.30, f32[2,1,3,32,128]{4,2,3,1,0:T(4,128)S(1)} %get-tuple-element.964, s32[]{:T(128)} %get-tuple-element.938, f32[32,128]{1,0:T(8,128)S(1)} %dynamic-slice_bitcast_fusion.32, f32[32,128]{1,0:T(8,128)S(1)} %broadcast_multiply_fusion.5, ...), kind=kOutput, calls=%fused_computation.93.clone.1 | convolution fusion | flops 58222848 | bytes 125445 | tf_op jit(solution)/shard_map/while/body/eval_jaxpr/kre,bckr->bce/dot_general | solution.py:86
  136.1 3.4 %fusion.286 = f32[32,128,128]{2,1,0:T(8,128)S(1)} fusion(f32[2,8,1,32,128]{4,1,3,2,0:T(8,128)S(1)} %get-tuple-element.959, s32[]{:T(128)} %get-tuple-element.938, f32[8,128]{1,0:T(8,128)S(1)} %get-tuple-element.960), kind=kOutput, calls=%fused_computation.99.clone.1 | convolution fusion | flops 50331648 | bytes 2232324 | tf_op jit(solution)/shard_map/while/body/eval_jaxpr/nbkr,nc->bkrc/dot_general | solution.py:78
  139.6 5.1 %fusion.287 = f32[1,384,128]{1,2,0:T(8,128)} fusion(s32[32,128]{1,0:T(8,128)S(1)} %dynamic-slice_bitcast_fusion.30, f32[32,128,128]{2,1,0:T(8,128)S(1)} %fusion.286, f32[128,128]{1,0:T(8,128)S(1)} %dynamic-slice_bitcast_fusion.31, f32[32,128]{1,0:T(8,128)S(1)} %multiply_bitcast_fusion.5, f32[1,384,128]{1,2,0:T(8,128)} %get-tuple-element.939, ...), kind=kOutput, calls=%fused_computation.87.clone.1 | convolution fusion | flops 2418638848 | bytes 2588673 | tf_op jit(solution)/shard_map/while/body/eval_jaxpr/kre,bkrc->bec/dot_general | solution.py:91
  144.7 3.2 %fusion.288 = f32[32,128,128]{2,1,0:T(8,128)S(1)} fusion(s32[32,128]{1,0:T(8,128)S(1)} %dynamic-slice_bitcast_fusion.30, f32[1,384,128]{2,1,0:T(8,128)S(1)} %get-tuple-element.962), kind=kOutput, calls=%fused_computation.75.clone.1 | convolution fusion | flops 2417491968 | bytes 2310144 | tf_op jit(solution)/shard_map/while/body/eval_jaxpr/kre,bec->bkrc/dot_general | solution.py:80
  147.9 2.4 %fusion.289 = f32[32,128]{1,0:T(8,128)S(1)} fusion(f32[32,128,128]{2,1,0:T(8,128)S(1)} %fusion.288, f32[128,128]{1,0:T(8,128)S(1)} %dynamic-slice_bitcast_fusion.31, f32[32,128]{1,0:T(8,128)S(1)} %multiply_bitcast_fusion.5, f32[2,8,1,32,128]{4,1,3,2,0:T(8,128)S(1)} %get-tuple-element.963, s32[]{:T(128)} %get-tuple-element.938, ...), kind=kOutput, calls=%fused_computation.91.clone.1 | convolution fusion | flops 51474432 | bytes 2461700 | tf_op jit(solution)/shard_map/while/body/eval_jaxpr/bkrc,nc->nbkr/dot_general | solution.py:83
  150.3 2.2 %fusion.290 = f32[1,3,384]{2,1,0:T(4,128)S(1)} fusion(s32[32,128]{1,0:T(8,128)S(1)} %dynamic-slice_bitcast_fusion.30, f32[2,1,3,32,128]{4,2,3,1,0:T(4,128)S(1)} %get-tuple-element.964, s32[]{:T(128)} %get-tuple-element.938, f32[32,128]{1,0:T(8,128)S(1)} %dynamic-slice_bitcast_fusion.32, f32[32,128]{1,0:T(8,128)S(1)} %broadcast_multiply_fusion.5, ...), kind=kOutput, calls=%fused_computation.93.clone.1 | convolution fusion | flops 58222848 | bytes 125445 | tf_op jit(solution)/shard_map/while/body/eval_jaxpr/kre,bckr->bce/dot_general | solution.py:86
  152.6 1.0 fusion.197
  154.4 0.8 collective-permute-done.4
  155.2 4.6 %collective-permute-done.5 = f32[1,64,128]{1,2,0:T(8,128)S(1)} collective-permute-done((f32[1,64,128]{1,2,0:T(8,128)S(1)}, f32[1,64,128]{1,2,0:T(8,128)S(1)}, u32[]{:S(2)}, u32[]{:S(2)}) %collective-permute-start.5) | collective-permute-done | bytes 32800 | tf_op jit(solution)/shard_map/ppermute | solution.py:24
  159.8 1.2 fusion.114
  161.0 1.3 fusion.112
  162.3 1.1 convolution_bitcast_fusion.1
  163.5 16.0 %while.61 = (s32[]{:T(128)}, f32[1,3,384]{2,1,0:T(4,128)S(1)}, f32[2,1,3,128]{3,2,1,0:T(4,128)S(1)}, f32[2,32,128]{2,1,0:T(8,128)S(1)}, f32[2,1,128,128]{3,2,1,0...) while((s32[]{:T(128)}, f32[1,3,384]{2,1,0:T(4,128)S(1)}, ...), condition=%wide.region_14.15_spmd, body=%wide.region_11.14_spmd.sunk | while | flops 2527233024 | bytes 5247133 | solution.py:219
  163.5 3.3 %fusion.275 = f32[32,128,128]{2,1,0:T(8,128)S(1)} fusion(s32[32,128]{1,0:T(8,128)S(1)} %dynamic-slice_bitcast_fusion.27, f32[1,384,128]{2,1,0:T(8,128)S(1)} %get-tuple-element.1000), kind=kOutput, calls=%fused_computation.41.clone.1 | convolution fusion | flops 2417491968 | bytes 2310144 | tf_op jit(solution)/shard_map/while/body/eval_jaxpr/kre,bec->bkrc/dot_general | solution.py:80
  166.8 2.3 %fusion.276 = f32[32,128]{1,0:T(8,128)S(1)} fusion(f32[32,128,128]{2,1,0:T(8,128)S(1)} %fusion.275, f32[128,128]{1,0:T(8,128)S(1)} %dynamic-slice_bitcast_fusion.29, f32[32,128]{1,0:T(8,128)S(1)} %multiply_bitcast_fusion.4, f32[2,8,1,32,128]{4,1,3,2,0:T(8,128)S(1)} %get-tuple-element.1003, s32[]{:T(128)} %get-tuple-element.981, ...), kind=kOutput, calls=%fused_computation.51.clone.1 | convolution fusion | flops 51474432 | bytes 2461700 | tf_op jit(solution)/shard_map/while/body/eval_jaxpr/bkrc,nc->nbkr/dot_general | solution.py:83
  169.3 2.2 %fusion.277 = f32[1,3,384]{2,1,0:T(4,128)S(1)} fusion(f32[1,3,384]{2,1,0:T(4,128)S(1)} %get-tuple-element.982, s32[32,128]{1,0:T(8,128)S(1)} %dynamic-slice_bitcast_fusion.27, f32[2,1,3,32,128]{4,2,3,1,0:T(4,128)S(1)} %get-tuple-element.1004, s32[]{:T(128)} %get-tuple-element.981, f32[32,128]{1,0:T(8,128)S(1)} %dynamic-slice_bitcast_fusion.28, ...), kind=kOutput, calls=%fused_computation.53.clone.1 | convolution fusion | flops 58221696 | bytes 125444 | tf_op jit(solution)/shard_map/while/body/eval_jaxpr/kre,bckr->bce/dot_general | solution.py:86
  171.5 3.3 %fusion.275 = f32[32,128,128]{2,1,0:T(8,128)S(1)} fusion(s32[32,128]{1,0:T(8,128)S(1)} %dynamic-slice_bitcast_fusion.27, f32[1,384,128]{2,1,0:T(8,128)S(1)} %get-tuple-element.1000), kind=kOutput, calls=%fused_computation.41.clone.1 | convolution fusion | flops 2417491968 | bytes 2310144 | tf_op jit(solution)/shard_map/while/body/eval_jaxpr/kre,bec->bkrc/dot_general | solution.py:80
  174.8 2.3 %fusion.276 = f32[32,128]{1,0:T(8,128)S(1)} fusion(f32[32,128,128]{2,1,0:T(8,128)S(1)} %fusion.275, f32[128,128]{1,0:T(8,128)S(1)} %dynamic-slice_bitcast_fusion.29, f32[32,128]{1,0:T(8,128)S(1)} %multiply_bitcast_fusion.4, f32[2,8,1,32,128]{4,1,3,2,0:T(8,128)S(1)} %get-tuple-element.1003, s32[]{:T(128)} %get-tuple-element.981, ...), kind=kOutput, calls=%fused_computation.51.clone.1 | convolution fusion | flops 51474432 | bytes 2461700 | tf_op jit(solution)/shard_map/while/body/eval_jaxpr/bkrc,nc->nbkr/dot_general | solution.py:83
  177.2 2.2 %fusion.277 = f32[1,3,384]{2,1,0:T(4,128)S(1)} fusion(f32[1,3,384]{2,1,0:T(4,128)S(1)} %get-tuple-element.982, s32[32,128]{1,0:T(8,128)S(1)} %dynamic-slice_bitcast_fusion.27, f32[2,1,3,32,128]{4,2,3,1,0:T(4,128)S(1)} %get-tuple-element.1004, s32[]{:T(128)} %get-tuple-element.981, f32[32,128]{1,0:T(8,128)S(1)} %dynamic-slice_bitcast_fusion.28, ...), kind=kOutput, calls=%fused_computation.53.clone.1 | convolution fusion | flops 58221696 | bytes 125444 | tf_op jit(solution)/shard_map/while/body/eval_jaxpr/kre,bckr->bce/dot_general | solution.py:86
  180.0 0.7 collective-permute-done.6
  180.7 4.0 %collective-permute-done.7 = f32[1,3,64]{2,1,0:T(4,128)S(1)} collective-permute-done((f32[1,3,64]{2,1,0:T(4,128)S(1)}, f32[1,3,64]{2,1,0:T(4,128)S(1)}, u32[]{:S(2)}, u32[]{:S(2)}) %collective-permute-start.7) | collective-permute-done | bytes 800 | tf_op jit(solution)/shard_map/ppermute | solution.py:24
  184.9 0.7 stack.2
  185.6 3.5 %all-to-all-start = ((f32[16,1,3,256]{3,1,2,0:T(1,128)}), f32[16,1,3,256]{3,1,2,0:T(1,128)S(1)}, u32[]{:S(2)}, u32[]{:S(2)}) async-start(f32[16,1,3,256]{3,1,2,0:T(1,128)} %stack.2), calls=%async_computation | async-start | bytes 98304 | tf_op jit(solution)/shard_map/all_to_all | solution.py:247
  189.1 8.9 %all-to-all-done = f32[16,1,3,256]{3,1,2,0:T(1,128)S(1)} async-done(((f32[16,1,3,256]{3,1,2,0:T(1,128)}), f32[16,1,3,256]{3,1,2,0:T(1,128)S(1)}, u32[]{:S(2)}, u32[]{:S(2)}) %all-to-all-start) | async-done | bytes 49184 | tf_op jit(solution)/shard_map/all_to_all | solution.py:247
  198.0 0.9 convolution_multiply_fusion
  (100 shorter events, 8.4 us)
Async XLA Ops:
  0.0 54.9 %copy-start = (f32[2,128]{1,0:T(2,128)S(1)}, f32[2,128]{1,0:T(2,128)}, u32[]{:S(2)}) copy-start(f32[2,128]{1,0:T(2,128)} %param.27) | copy-start | bytes 3076
  44.7 12.0 %collective-permute-start = (f32[1,4,64]{2,1,0:T(4,128)S(1)}, f32[1,4,64]{2,1,0:T(4,128)S(1)}, u32[]{:S(2)}, u32[]{:S(2)}) collective-permute-start(f32[1,4,64]{2,1,0:T(4,128)S(1)} %get-tuple-element.595), channel_id=1, source_target_pairs={{0,1},{1,2},{2,3},{3,4},{4,5},{5,6},{6,7},{7,8},{8,9},{9,10},{10,1... | collective-permute-start | bytes 3080 | tf_op jit(solution)/shard_map/ppermute | solution.py:21
  52.8 5.1 %collective-permute-start.1 = (f32[1,4,64]{2,1,0:T(4,128)S(1)}, f32[1,4,64]{2,1,0:T(4,128)S(1)}, u32[]{:S(2)}, u32[]{:S(2)}) collective-permute-start(f32[1,4,64]{2,1,0:T(4,128)S(1)} %get-tuple-element.596), channel_id=1, source_target_pairs={{1,0},{2,1},{3,2},{4,3},{5,4},{6,5},{7,6},{8,7},{9,8},{10,9},{11,1... | collective-permute-start | bytes 3080 | tf_op jit(solution)/shard_map/ppermute | solution.py:24
  66.1 19.7 %copy-start.1 = (f32[2,128,128]{2,1,0:T(8,128)S(1)}, f32[2,128,128]{2,1,0:T(8,128)}, u32[]{:S(2)}) copy-start(f32[2,128,128]{2,1,0:T(8,128)} %param.30) | copy-start | bytes 393220
  66.1 20.7 %copy-start.3 = (s32[256]{0:T(256)S(1)}, s32[256]{0:T(256)}, u32[]{:S(2)}) copy-start(s32[256]{0:T(256)} %param.23) | copy-start | bytes 3076
  66.1 22.1 %copy-start.4 = (s32[128]{0:T(128)S(1)}, s32[128]{0:T(128)}, u32[]{:S(2)}) copy-start(s32[128]{0:T(128)} %param.26) | copy-start | bytes 1540
  86.1 0.7 copy-start.2
  88.4 3.8 %collective-permute-start.2 = (f32[1,64,128]{2,1,0:T(8,128)S(1)}, f32[1,64,128]{2,1,0:T(8,128)S(1)}, u32[]{:S(2)}, u32[]{:S(2)}) collective-permute-start(f32[1,64,128]{2,1,0:T(8,128)S(1)} %get-tuple-element.580), channel_id=1, source_target_pairs={{0,1},{1,2},{2,3},{3,4},{4,5},{5,6},{6,7},{7,8},{8,9},{9,10},{10,1... | collective-permute-start | bytes 98312 | tf_op jit(solution)/shard_map/ppermute | solution.py:21
  91.2 6.0 %collective-permute-start.3 = (f32[1,64,128]{2,1,0:T(8,128)S(1)}, f32[1,64,128]{2,1,0:T(8,128)S(1)}, u32[]{:S(2)}, u32[]{:S(2)}) collective-permute-start(f32[1,64,128]{2,1,0:T(8,128)S(1)} %get-tuple-element.581), channel_id=1, source_target_pairs={{1,0},{2,1},{3,2},{4,3},{5,4},{6,5},{7,6},{8,7},{9,8},{10,9},{11,1... | collective-permute-start | bytes 98312 | tf_op jit(solution)/shard_map/ppermute | solution.py:24
  97.8 20.9 %copy-start.5 = (f32[128]{0:T(128)S(1)}, f32[128]{0:T(128)}, u32[]{:S(2)}) copy-start(f32[128]{0:T(128)} %param.31) | copy-start | bytes 1540
  153.6 1.6 collective-permute-start.4
  153.9 5.9 %collective-permute-start.5 = (f32[1,64,128]{1,2,0:T(8,128)S(1)}, f32[1,64,128]{1,2,0:T(8,128)S(1)}, u32[]{:S(2)}, u32[]{:S(2)}) collective-permute-start(f32[1,64,128]{1,2,0:T(8,128)S(1)} %get-tuple-element.579), channel_id=1, source_target_pairs={{1,0},{2,1},{3,2},{4,3},{5,4},{6,5},{7,6},{8,7},{9,8},{10,9},{11,1... | collective-permute-start | bytes 98312 | tf_op jit(solution)/shard_map/ppermute | solution.py:24
  179.5 1.2 collective-permute-start.6
  179.6 5.2 %collective-permute-start.7 = (f32[1,3,64]{2,1,0:T(4,128)S(1)}, f32[1,3,64]{2,1,0:T(4,128)S(1)}, u32[]{:S(2)}, u32[]{:S(2)}) collective-permute-start(f32[1,3,64]{2,1,0:T(4,128)S(1)} %get-tuple-element.589), channel_id=1, source_target_pairs={{1,0},{2,1},{3,2},{4,3},{5,4},{6,5},{7,6},{8,7},{9,8},{10,9},{11,1... | collective-permute-start | bytes 2312 | tf_op jit(solution)/shard_map/ppermute | solution.py:24
  185.6 12.4 %all-to-all-start = ((f32[16,1,3,256]{3,1,2,0:T(1,128)}), f32[16,1,3,256]{3,1,2,0:T(1,128)S(1)}, u32[]{:S(2)}, u32[]{:S(2)}) async-start(f32[16,1,3,256]{3,1,2,0:T(1,128)} %stack.2), calls=%async_computation | async-start | bytes 98304 | tf_op jit(solution)/shard_map/all_to_all | solution.py:247
